TPU v7x, 32 devices: a whole 2x2x4 slice. The times are simulated.
32 devices in a mesh: dp: 8 (over z, x), tensor: 4 (over y, core).
Axes of the slice: x: 2, y: 2, z: 4, core: 2. Of those that a mesh axis runs over, the one named last changes fastest.
Arguments:
- tokens: bfloat16 [32768, 768], P(('dp', 'tensor')), may hold values from -6 to 6
- lengths: int32 [32], P('dp'), may hold values from 256 to 1024, as said below
- w_query: bfloat16 [768, 768], P('dp', 'tensor'), may hold values from -0.3125 to 0.3125
- w_key: bfloat16 [768, 768], P('dp', 'tensor'), may hold values from -0.3125 to 0.3125
- w_value: bfloat16 [768, 768], P('dp', 'tensor'), may hold values from -0.21875 to 0.21875
- w_out: bfloat16 [768, 768], P('tensor', 'dp'), may hold values from -1 to 1
- w_up: bfloat16 [768, 3072], P('dp', 'tensor'), may hold values from -0.21875 to 0.21875
- w_down: bfloat16 [3072, 768], P('tensor', 'dp'), may hold values from -0.109375 to 0.109375
- query_bias: float32 [768], P(('dp', 'tensor')), may hold values from -1.8 to 1.8
- value_bias: float32 [768], P(('dp', 'tensor')), may hold values from -1.8 to 1.8
- out_bias: float32 [768], P(('dp', 'tensor')), may hold values from -1.2 to 1.2
- attn_gain: float32 [768], P(('dp', 'tensor')), may hold values from 0.25 to 1.75
- attn_shift: float32 [768], P(('dp', 'tensor')), may hold values from -1.2 to 1.2
- up_bias: float32 [3072], P(('dp', 'tensor')), may hold values from -1.8 to 1.8
- down_bias: float32 [768], P(('dp', 'tensor')), may hold values from -1.2 to 1.2
- ffn_gain: float32 [768], P(('dp', 'tensor')), may hold values from 0.25 to 1.75
- ffn_shift: float32 [768], P(('dp', 'tensor')), may hold values from -1.8 to 1.8
- cotangent: bfloat16 [32768, 768], P(('dp', 'tensor')), may hold values from -6 to 6
Outputs:
- output: float32 [32768, 768], P(('dp', 'tensor'))
- grad_tokens: float32 [32768, 768], P(('dp', 'tensor'))
- query_grad: float32 [768, 768], P('dp', 'tensor')
- key_grad: float32 [768, 768], P('dp', 'tensor')
- value_grad: float32 [768, 768], P('dp', 'tensor')
- out_grad: float32 [768, 768], P('tensor', 'dp')
- up_grad: float32 [768, 3072], P('dp', 'tensor')
- down_grad: float32 [3072, 768], P('tensor', 'dp')
- query_bias_grad: float32 [768], P(('dp', 'tensor'))
- value_bias_grad: float32 [768], P(('dp', 'tensor'))
- out_bias_grad: float32 [768], P(('dp', 'tensor'))
- attn_gain_grad: float32 [768], P(('dp', 'tensor'))
- attn_shift_grad: float32 [768], P(('dp', 'tensor'))
- up_bias_grad: float32 [3072], P(('dp', 'tensor'))
- down_bias_grad: float32 [768], P(('dp', 'tensor'))
- ffn_gain_grad: float32 [768], P(('dp', 'tensor'))
- ffn_shift_grad: float32 [768], P(('dp', 'tensor'))
Inputs may be any that keep to these rules, and one draw needn't show every extreme that they name: `lengths`: each sequence's count of valid tokens, which come first in it; in every draw some sequence has all 1024 slots valid and some has 256.
All inputs are finite; a program needn't handle non-finite values.
Results may differ from a plain program's by a relative error of at most 0.019.
Values may be sent and summed in bfloat16 or wider, within the bound.
A program may use at most 192 MiB of HBM per device.

v0:
```python
import jax
import jax.numpy as jnp
from jax import lax
from jax.sharding import PartitionSpec as P

HEAD = 64
EPSILON = 1e-12
FLOOR_SCORE = -1e30


def cut_along(shard, dim, peers):
    before, after = (shard.shape[:dim], shard.shape[dim + 1 :])
    return jnp.moveaxis(shard.reshape(*before, peers, -1, *after), dim, 0)


def sum_at_owner(shard, axis, dim):
    parts = cut_along(shard, dim, lax.axis_size(axis))
    arrived = lax.all_to_all(parts, axis, split_axis=0, concat_axis=0, tiled=True)
    return arrived.astype(jnp.float32).sum(axis=0)


def side_by_side(arrays, axis, dim, along):
    widths = [a.shape[along] for a in arrays]
    both = jnp.concatenate(arrays, axis=along)
    whole = sum_at_owner(both, axis, dim)
    return tuple(jnp.split(whole, [sum(widths[:k]) for k in range(1, len(widths))], axis=along))


def matmul(left_side, right_side):
    return jnp.dot(left_side, right_side, preferred_element_type=jnp.float32)


def contract_rows(left_side, right_side):
    return lax.dot_general(
        left_side, right_side, (((0,), (0,)), ((), ())), preferred_element_type=jnp.float32
    )


def contract_cols(left_side, right_side):
    return lax.dot_general(
        left_side, right_side, (((1,), (1,)), ((), ())), preferred_element_type=jnp.float32
    )


def round_trip(operand):
    return lax.optimization_barrier(operand.astype(jnp.bfloat16)).astype(jnp.float32)


def layer_norm(values, norm_gain, norm_shift):
    center = values - jnp.mean(values, axis=-1, keepdims=True)
    spread = jnp.mean(center * center, axis=-1, keepdims=True)
    return center * lax.rsqrt(spread + EPSILON) * norm_gain + norm_shift


def gelu_exact(values):
    return jax.nn.gelu(values, approximate=False)


def head_scores(query_seq, key_seq, length):
    scores = jnp.einsum(
        "qhd,khd->hqk", query_seq, key_seq, preferred_element_type=jnp.float32
    ) * HEAD ** (-0.5)
    counted = jnp.arange(key_seq.shape[0], dtype=jnp.int32) < length
    return (jnp.where(counted[None, None, :], scores, FLOOR_SCORE), counted)


def attend_forward(seq_items):
    query_seq, key_seq, value_seq, length = seq_items
    scores, counted = head_scores(query_seq, key_seq, length)
    row_top = jnp.max(scores, axis=-1, keepdims=True)
    exp_terms = jnp.exp(scores - row_top)
    row_total = jnp.sum(exp_terms, axis=-1, keepdims=True)
    prob_low = (exp_terms / row_total).astype(jnp.bfloat16)
    head_mix = jnp.einsum("hqk,khd->qhd", prob_low, value_seq, preferred_element_type=jnp.float32)
    return (head_mix.astype(jnp.bfloat16), (row_top + jnp.log(row_total))[..., 0])


def attend_backward(seq_items):
    query_seq, key_seq, value_seq, length, log_total, grad_mix = seq_items
    scores, counted = head_scores(query_seq, key_seq, length)
    prob_full = jnp.exp(scores - log_total[..., None])
    prob_low = prob_full.astype(jnp.bfloat16)
    grad_value = jnp.einsum("hqk,qhd->khd", prob_low, grad_mix, preferred_element_type=jnp.float32)
    grad_probs = jnp.einsum("qhd,khd->hqk", grad_mix, value_seq, preferred_element_type=jnp.float32)
    row_inner = jnp.sum(prob_full * grad_probs, axis=-1, keepdims=True)
    grad_scores = jnp.where(
        counted[None, None, :], prob_full * (grad_probs - row_inner), 0.0
    ).astype(jnp.bfloat16)
    score_scale = HEAD ** (-0.5)
    grad_query = (
        jnp.einsum("hqk,khd->qhd", grad_scores, key_seq, preferred_element_type=jnp.float32)
        * score_scale
    )
    grad_key = (
        jnp.einsum("hqk,qhd->khd", grad_scores, query_seq, preferred_element_type=jnp.float32)
        * score_scale
    )
    return (
        grad_query.astype(jnp.bfloat16),
        grad_key.astype(jnp.bfloat16),
        grad_value.astype(jnp.bfloat16),
    )


def shards(
    tokens,
    lengths,
    w_query,
    w_key,
    w_value,
    w_out,
    w_up,
    w_down,
    query_bias,
    value_bias,
    out_bias,
    attn_gain,
    attn_shift,
    up_bias,
    down_bias,
    ffn_gain,
    ffn_shift,
    cotangent,
):
    tensor_rank = lax.axis_index("tensor")
    small_full = (
        lax.all_gather(query_bias, ("dp", "tensor"), axis=0, tiled=True),
        lax.all_gather(value_bias, ("dp", "tensor"), axis=0, tiled=True),
        lax.all_gather(out_bias, ("dp", "tensor"), axis=0, tiled=True),
        lax.all_gather(attn_gain, ("dp", "tensor"), axis=0, tiled=True),
        lax.all_gather(attn_shift, ("dp", "tensor"), axis=0, tiled=True),
        lax.all_gather(up_bias, ("dp", "tensor"), axis=0, tiled=True),
        lax.all_gather(down_bias, ("dp", "tensor"), axis=0, tiled=True),
        lax.all_gather(ffn_gain, ("dp", "tensor"), axis=0, tiled=True),
        lax.all_gather(ffn_shift, ("dp", "tensor"), axis=0, tiled=True),
    )
    (
        qbias_full,
        vbias_full,
        obias_full,
        gain_one,
        shift_one,
        ubias_full,
        dbias_full,
        gain_two,
        shift_two,
    ) = small_full
    query_weight, key_weight, value_weight, out_weight, up_weight, down_weight = (
        lax.all_gather(w_query, "dp", axis=0, tiled=True),
        lax.all_gather(w_key, "dp", axis=0, tiled=True),
        lax.all_gather(w_value, "dp", axis=0, tiled=True),
        lax.all_gather(w_out, "dp", axis=1, tiled=True),
        lax.all_gather(w_up, "dp", axis=0, tiled=True),
        lax.all_gather(w_down, "dp", axis=1, tiled=True),
    )
    row_count = tokens.shape[0]
    model_width = tokens.shape[1]
    head_cols = query_weight.shape[1]
    local_heads = head_cols // HEAD
    seq_count = lengths.shape[0]
    group_total = row_count * lax.axis_size("tensor")
    seq_len = group_total // seq_count
    head_offset = tensor_rank * head_cols

    def to_heads(matrix):
        return matrix.reshape(seq_count, seq_len, local_heads, HEAD)

    group_rows = lax.all_gather(tokens, "tensor", axis=0, tiled=True)
    query_shift = lax.dynamic_slice_in_dim(qbias_full, head_offset, head_cols)
    value_shift = lax.dynamic_slice_in_dim(vbias_full, head_offset, head_cols)
    queries = (matmul(group_rows, query_weight) + query_shift).astype(jnp.bfloat16)
    keys_low = matmul(group_rows, key_weight).astype(jnp.bfloat16)
    values_low = (matmul(group_rows, value_weight) + value_shift).astype(jnp.bfloat16)
    head_mix, log_totals = lax.map(
        attend_forward, (to_heads(queries), to_heads(keys_low), to_heads(values_low), lengths)
    )
    mixed_rows = head_mix.reshape(group_total, head_cols)
    attention = (
        lax.psum_scatter(
            matmul(mixed_rows, out_weight).astype(jnp.bfloat16),
            "tensor",
            scatter_dimension=0,
            tiled=True,
        ).astype(jnp.float32)
        + obias_full
    )
    residual_one = tokens.astype(jnp.float32) + attention
    hidden, norm_one_back = jax.vjp(layer_norm, residual_one, gain_one, shift_one)
    hidden_low = hidden.astype(jnp.bfloat16)
    unit_cols = up_weight.shape[1]
    ffn_rows = lax.all_gather(hidden_low, "tensor", axis=0, tiled=True)
    up_shift = lax.dynamic_slice_in_dim(ubias_full, tensor_rank * unit_cols, unit_cols)
    pre_act = matmul(ffn_rows, up_weight) + up_shift
    act_full, gelu_back = jax.vjp(gelu_exact, pre_act)
    act_low = act_full.astype(jnp.bfloat16)
    branch = (
        lax.psum_scatter(
            matmul(act_low, down_weight).astype(jnp.bfloat16),
            "tensor",
            scatter_dimension=0,
            tiled=True,
        ).astype(jnp.float32)
        + dbias_full
    )
    residual_two = hidden + branch
    normed, norm_two_back = jax.vjp(layer_norm, residual_two, gain_two, shift_two)
    positions = tensor_rank * row_count + jnp.arange(row_count, dtype=jnp.int32)
    seq_of_row = positions // seq_len
    row_length = jnp.sum(
        jnp.where(
            seq_of_row[:, None] == jnp.arange(seq_count, dtype=jnp.int32)[None, :],
            lengths[None, :],
            0,
        ),
        axis=1,
    )
    valid = (positions % seq_len < row_length).astype(jnp.float32)[:, None]
    output = normed * valid
    grad_second, ffn_gain_grad, ffn_shift_grad = norm_two_back(
        cotangent.astype(jnp.float32) * valid
    )
    grad_branch = grad_second.astype(jnp.bfloat16)
    down_bias_grad = jnp.sum(grad_branch.astype(jnp.float32), axis=0)
    branch_rows = lax.all_gather(grad_branch, "tensor", axis=0, tiled=True)
    grad_act = contract_cols(branch_rows, down_weight).astype(jnp.bfloat16)
    down_grad = contract_rows(act_low, branch_rows)
    grad_pre = gelu_back(grad_act.astype(jnp.float32))[0].astype(jnp.bfloat16)
    up_grad = contract_rows(ffn_rows, grad_pre)
    up_part = jnp.sum(grad_pre.astype(jnp.float32), axis=0)
    up_bias_grad = lax.dynamic_update_slice_in_dim(
        jnp.zeros(ubias_full.shape, jnp.float32), up_part, tensor_rank * unit_cols, 0
    )
    grad_from_ffn = lax.psum_scatter(
        contract_cols(grad_pre, up_weight).astype(jnp.bfloat16),
        "tensor",
        scatter_dimension=0,
        tiled=True,
    ).astype(jnp.float32)
    grad_hidden = grad_second + round_trip(grad_from_ffn)
    grad_first, attn_gain_grad, attn_shift_grad = norm_one_back(grad_hidden)
    grad_attn = grad_first.astype(jnp.bfloat16)
    out_bias_grad = jnp.sum(grad_attn.astype(jnp.float32), axis=0)
    attn_grad_rows = lax.all_gather(grad_attn, "tensor", axis=0, tiled=True)
    grad_mixed = contract_cols(attn_grad_rows, out_weight).astype(jnp.bfloat16)
    out_grad = contract_rows(mixed_rows, attn_grad_rows)
    grad_queries, grad_keys, grad_values = lax.map(
        attend_backward,
        (
            to_heads(queries),
            to_heads(keys_low),
            to_heads(values_low),
            lengths,
            log_totals,
            to_heads(grad_mixed),
        ),
    )
    grad_queries = grad_queries.reshape(group_total, head_cols)
    grad_keys = grad_keys.reshape(group_total, head_cols)
    grad_values = grad_values.reshape(group_total, head_cols)
    query_grad = contract_rows(group_rows, grad_queries)
    key_grad = contract_rows(group_rows, grad_keys)
    value_grad = contract_rows(group_rows, grad_values)
    blank_width = jnp.zeros((model_width,), jnp.float32)
    query_bias_grad = lax.dynamic_update_slice_in_dim(
        blank_width, jnp.sum(grad_queries.astype(jnp.float32), axis=0), head_offset, 0
    )
    value_bias_grad = lax.dynamic_update_slice_in_dim(
        blank_width, jnp.sum(grad_values.astype(jnp.float32), axis=0), head_offset, 0
    )
    input_part = (
        contract_cols(grad_queries, query_weight)
        + contract_cols(grad_keys, key_weight)
        + contract_cols(grad_values, value_weight)
    )
    grad_tokens = grad_first + lax.psum_scatter(
        input_part.astype(jnp.bfloat16), "tensor", scatter_dimension=0, tiled=True
    ).astype(jnp.float32)
    owned = (
        *side_by_side(
            (
                query_grad.astype(jnp.bfloat16),
                key_grad.astype(jnp.bfloat16),
                value_grad.astype(jnp.bfloat16),
            ),
            "dp",
            0,
            1,
        ),
        sum_at_owner(out_grad.astype(jnp.bfloat16), "dp", 1),
        sum_at_owner(up_grad.astype(jnp.bfloat16), "dp", 0),
        sum_at_owner(down_grad.astype(jnp.bfloat16), "dp", 1),
    )
    small_owned = (
        lax.psum_scatter(query_bias_grad, ("dp", "tensor"), scatter_dimension=0, tiled=True),
        lax.psum_scatter(value_bias_grad, ("dp", "tensor"), scatter_dimension=0, tiled=True),
        lax.psum_scatter(out_bias_grad, ("dp", "tensor"), scatter_dimension=0, tiled=True),
        lax.psum_scatter(attn_gain_grad, ("dp", "tensor"), scatter_dimension=0, tiled=True),
        lax.psum_scatter(attn_shift_grad, ("dp", "tensor"), scatter_dimension=0, tiled=True),
        lax.psum_scatter(up_bias_grad, ("dp", "tensor"), scatter_dimension=0, tiled=True),
        lax.psum_scatter(down_bias_grad, ("dp", "tensor"), scatter_dimension=0, tiled=True),
        lax.psum_scatter(ffn_gain_grad, ("dp", "tensor"), scatter_dimension=0, tiled=True),
        lax.psum_scatter(ffn_shift_grad, ("dp", "tensor"), scatter_dimension=0, tiled=True),
    )
    return (
        output,
        grad_tokens,
        owned[0],
        owned[1],
        owned[2],
        owned[3],
        owned[4],
        owned[5],
        small_owned[0],
        small_owned[1],
        small_owned[2],
        small_owned[3],
        small_owned[4],
        small_owned[5],
        small_owned[6],
        small_owned[7],
        small_owned[8],
    )


def solution(mesh):
    placed = (
        P(("dp", "tensor"), None),
        P("dp"),
        P("dp", "tensor"),
        P("dp", "tensor"),
        P("dp", "tensor"),
        P("tensor", "dp"),
        P("dp", "tensor"),
        P("tensor", "dp"),
        P(("dp", "tensor")),
        P(("dp", "tensor")),
        P(("dp", "tensor")),
        P(("dp", "tensor")),
        P(("dp", "tensor")),
        P(("dp", "tensor")),
        P(("dp", "tensor")),
        P(("dp", "tensor")),
        P(("dp", "tensor")),
        P(("dp", "tensor"), None),
    )
    return jax.shard_map(
        shards,
        mesh=mesh,
        in_specs=placed,
        out_specs=(
            P(("dp", "tensor"), None),
            P(("dp", "tensor"), None),
            P("dp", "tensor"),
            P("dp", "tensor"),
            P("dp", "tensor"),
            P("tensor", "dp"),
            P("dp", "tensor"),
            P("tensor", "dp"),
            P(("dp", "tensor")),
            P(("dp", "tensor")),
            P(("dp", "tensor")),
            P(("dp", "tensor")),
            P(("dp", "tensor")),
            P(("dp", "tensor")),
            P(("dp", "tensor")),
            P(("dp", "tensor")),
            P(("dp", "tensor")),
        ),
        check_vma=False,
    )
```

profile of v0, /device:TPU:0, one launch (start us, length us, event | category | flops | bytes accessed | tf_op | source)
XLA Modules:
  0.0 1138.1 jit_solution(15248481869915932841)
XLA Ops:
  15.5 44.0 %all-reduce.19 = (f32[768]{0:T(1024)}, f32[768]{0:T(1024)}, f32[768]{0:T(1024)S(1)}, f32[768]{0:T(1024)S(1)}, f32[768]{0:T(1024)S(1)}, /*index=5*/f32[3072]{0:T(1024)}, f32[768]{0:T(1024)}, f32[768]{0:T(1024)}) all-reduce(f32[768]{0:T(1024)S(1)} %dynamic-update-slice.4, ...), channel_id=1, replica_groups=mesh['dp'=8,'tensor'=4] {'dp','tensor'}, use_global_device_ids=true, to_apply=%add.4 | all-reduce | flops 8448 | bytes 67584
  60.6 31.0 %all_gather.63 = bf16[192,768]{0,1:T(8,128)(2,1)S(1)} all-gather(bf16[192,96]{0,1:T(8,128)(2,1)S(1)} %copy.88), channel_id=1, replica_groups=mesh['dp'=8,'tensor'=4] {'dp'}, dimensions={1}, use_global_device_ids=true | all-gather | bytes 331776 | tf_op jit(solution)/shard_map/all_gather | solution.py:152
  91.5 33.2 %all_gather.60 = bf16[768,192]{1,0:T(8,128)(2,1)} all-gather(bf16[96,192]{1,0:T(8,128)(2,1)} %param.24), channel_id=1, replica_groups=mesh['dp'=8,'tensor'=4] {'dp'}, dimensions={0}, use_global_device_ids=true | all-gather | bytes 331776 | tf_op jit(solution)/shard_map/all_gather | solution.py:149
  124.7 33.3 %all_gather.62 = bf16[768,192]{1,0:T(8,128)(2,1)} all-gather(bf16[96,192]{1,0:T(8,128)(2,1)} %param.25), channel_id=1, replica_groups=mesh['dp'=8,'tensor'=4] {'dp'}, dimensions={0}, use_global_device_ids=true | all-gather | bytes 331776 | tf_op jit(solution)/shard_map/all_gather | solution.py:150
  158.0 31.2 %all_gather.58 = bf16[768,192]{1,0:T(8,128)(2,1)S(1)} all-gather(bf16[96,192]{1,0:T(8,128)(2,1)S(1)} %copy-done.42), channel_id=1, replica_groups=mesh['dp'=8,'tensor'=4] {'dp'}, dimensions={0}, use_global_device_ids=true | all-gather | bytes 331776 | tf_op jit(solution)/shard_map/all_gather | solution.py:151
  215.6 49.6 %while.26 = (s32[]{:T(128)}, bf16[4,1024,3,64]{1,3,2,0:T(8,128)(2,1)}, f32[4,3,1024]{2,1,0:T(4,128)}, bf16[4,1024,3,64]{1,3,2,0:T(8,128)(2,1)}, s32[4]{0:T(128)S...) while((s32[]{:T(128)}, ...), condition=%wide.region_3.4_spmd, body=%wide.region_0.3_spmd.sunk | while | flops 843249664 | bytes 39430256 | solution.py:174
  276.3 58.1 %reduce-scatter.5.cloned.1.call-done = bf16[1024,768]{1,0:T(8,128)(2,1)} async-done(((bf16[4096,768]{1,0:T(8,128)(2,1)}), bf16[1024,768]{1,0:T(8,128)(2,1)}) %reduce-scatter.5.cloned.1.call-update) | async-done | bytes 1572880 | tf_op jit(solution)/shard_map/reduce_scatter | solution.py:179
  340.9 44.9 %all-gather.9.cloned.1.call-done = bf16[4096,768]{1,0:T(8,128)(2,1)} async-done(((bf16[1024,768]{1,0:T(8,128)(2,1)}), bf16[4096,768]{1,0:T(8,128)(2,1)}) %all-gather.9.cloned.1.call-update) | async-done | bytes 6291472 | tf_op jit(solution)/shard_map/all_gather | solution.py:191
  385.9 34.8 %multiply_convert_fusion = (bf16[4096,768]{1,0:T(8,128)(2,1)}, f32[4096,768]{1,0:T(8,128)}, f32[4096,768]{1,0:T(8,128)}) fusion(f32[768]{0:T(1024)S(1)} %dynamic_slice.44, bf16[4096,768]{1,0:T(8,128)(2,1)} %all-gather.9.cloned.1.call-done, bf16[768,768]{1,0:T(8,128)(2,1)} %all-gather.11.cloned.1.call-done), kind=kOutput, calls=%fused_computation.97 | convolution fusion | flops 5039456256 | bytes 38931456 | tf_op jit(solution)/shard_map/dot_general | solution.py:30
  420.7 8.6 all-gather.13.cloned.1.call-done
  429.3 9.2 convolution_convert_fusion.3
  438.9 56.9 %reduce-scatter.7.cloned.1.call-done = bf16[1024,768]{1,0:T(8,128)(2,1)} async-done(((bf16[4096,768]{1,0:T(8,128)(2,1)}), bf16[1024,768]{1,0:T(8,128)(2,1)}) %reduce-scatter.7.cloned.1.call-update) | async-done | bytes 1572880 | tf_op jit(solution)/shard_map/reduce_scatter | solution.py:197
  509.1 46.5 %all-gather.15.cloned.1.call-done = bf16[4096,768]{1,0:T(8,128)(2,1)} async-done(((bf16[1024,768]{1,0:T(8,128)(2,1)}), bf16[4096,768]{1,0:T(8,128)(2,1)}) %all-gather.15.cloned.1.call-update) | async-done | bytes 6291472 | tf_op jit(solution)/shard_map/all_gather | solution.py:224
  555.6 19.1 %convert_reduce_fusion = (f32[768]{0:T(1024)}, bf16[4096,768]{1,0:T(8,128)(2,1)}) fusion(f32[4096,768]{1,0:T(8,128)} %get-tuple-element.253, f32[4096,768]{1,0:T(8,128)} %get-tuple-element.259, f32[768]{0:T(1024)S(1)} %dynamic_slice.44, bf16[4096,768]{1,0:T(8,128)(2,1)} %all-gather.15.cloned.1.call-done, bf16[768,768]{0,1:T(8,128)(2,1)} %all-gather.13.cloned.1.call-done), kind=kOutput, calls=%fused_computation.95 | convolution fusion | flops 4891606016 | bytes 38934528 | tf_op jit(solution)/shard_map/dot_general | solution.py:40
  574.6 9.7 convolution_convert_fusion.1
  584.4 58.8 %reduce-scatter.9.cloned.1.call-done = bf16[1024,768]{1,0:T(8,128)(2,1)} async-done(((bf16[4096,768]{1,0:T(8,128)(2,1)}), bf16[1024,768]{1,0:T(8,128)(2,1)}) %reduce-scatter.9.cloned.1.call-update) | async-done | bytes 1572880 | tf_op jit(solution)/shard_map/reduce_scatter | solution.py:233
  653.9 46.5 %all-gather.17.cloned.1.call-done = bf16[4096,768]{1,0:T(8,128)(2,1)} async-done(((bf16[1024,768]{1,0:T(8,128)(2,1)}), bf16[4096,768]{1,0:T(8,128)(2,1)}) %all-gather.17.cloned.1.call-update) | async-done | bytes 6291472 | tf_op jit(solution)/shard_map/all_gather | solution.py:243
  712.4 220.9 %while.27 = (s32[]{:T(128)}, bf16[4,1024,3,64]{1,3,2,0:T(8,128)(2,1)}, bf16[4,1024,3,64]{1,3,2,0:T(8,128)(2,1)}, bf16[4,1024,3,64]{1,3,2,0:T(8,128)(2,1)}, bf16[...) while((s32[]{:T(128)}, ...), condition=%wide.region_18.19_spmd, body=%wide.region_16.18_spmd.sunk | while | flops 2096047104 | bytes 199085264 | solution.py:246
  728.6 19.8 %fusion.228 = bf16[4,1024,3,64]{1,3,2,0:T(8,128)(2,1)} fusion(bf16[4,1024,3,64]{1,3,2,0:T(8,128)(2,1)} %get-tuple-element.407, s32[]{:T(128)S(6)} %copy.135, f32[3,1024,1024]{1,2,0:T(8,128)} %fusion.225, f32[3,1024,1024]{1,2,0:T(8,128)} %copy-done, f32[3,1024]{1,0:T(4,128)S(1)} %dynamic-slice_bitcast_fusion.2, ...), kind=kOutput, calls=%fused_computation.52.clone.1 | convolution fusion | flops 437653504 | bytes 51153920 | tf_op jit(solution)/shard_map/while/body/eval_jaxpr/hqk,qhd->khd/dot_general | solution.py:95
  748.4 19.5 %fusion.227 = bf16[4,1024,3,64]{1,3,2,0:T(8,128)(2,1)} fusion(bf16[4,1024,3,64]{1,3,2,0:T(8,128)(2,1)} %get-tuple-element.406, s32[]{:T(128)S(6)} %copy.135, f32[3,1024,1024]{1,2,0:T(8,128)} %fusion.225, f32[3,1024,1024]{1,2,0:T(8,128)} %copy-done, f32[3,1024]{1,0:T(4,128)S(1)} %dynamic-slice_bitcast_fusion.2, ...), kind=kOutput, calls=%fused_computation.50.clone.1 | convolution fusion | flops 437653504 | bytes 51153920 | tf_op jit(solution)/shard_map/while/body/eval_jaxpr/hqk,khd->qhd/dot_general | solution.py:91
  783.7 19.8 %fusion.228 = bf16[4,1024,3,64]{1,3,2,0:T(8,128)(2,1)} fusion(bf16[4,1024,3,64]{1,3,2,0:T(8,128)(2,1)} %get-tuple-element.407, s32[]{:T(128)S(6)} %copy.135, f32[3,1024,1024]{1,2,0:T(8,128)} %fusion.225, f32[3,1024,1024]{1,2,0:T(8,128)} %copy-done, f32[3,1024]{1,0:T(4,128)S(1)} %dynamic-slice_bitcast_fusion.2, ...), kind=kOutput, calls=%fused_computation.52.clone.1 | convolution fusion | flops 437653504 | bytes 51153920 | tf_op jit(solution)/shard_map/while/body/eval_jaxpr/hqk,qhd->khd/dot_general | solution.py:95
  803.5 19.5 %fusion.227 = bf16[4,1024,3,64]{1,3,2,0:T(8,128)(2,1)} fusion(bf16[4,1024,3,64]{1,3,2,0:T(8,128)(2,1)} %get-tuple-element.406, s32[]{:T(128)S(6)} %copy.135, f32[3,1024,1024]{1,2,0:T(8,128)} %fusion.225, f32[3,1024,1024]{1,2,0:T(8,128)} %copy-done, f32[3,1024]{1,0:T(4,128)S(1)} %dynamic-slice_bitcast_fusion.2, ...), kind=kOutput, calls=%fused_computation.50.clone.1 | convolution fusion | flops 437653504 | bytes 51153920 | tf_op jit(solution)/shard_map/while/body/eval_jaxpr/hqk,khd->qhd/dot_general | solution.py:91
  838.8 19.8 %fusion.228 = bf16[4,1024,3,64]{1,3,2,0:T(8,128)(2,1)} fusion(bf16[4,1024,3,64]{1,3,2,0:T(8,128)(2,1)} %get-tuple-element.407, s32[]{:T(128)S(6)} %copy.135, f32[3,1024,1024]{1,2,0:T(8,128)} %fusion.225, f32[3,1024,1024]{1,2,0:T(8,128)} %copy-done, f32[3,1024]{1,0:T(4,128)S(1)} %dynamic-slice_bitcast_fusion.2, ...), kind=kOutput, calls=%fused_computation.52.clone.1 | convolution fusion | flops 437653504 | bytes 51153920 | tf_op jit(solution)/shard_map/while/body/eval_jaxpr/hqk,qhd->khd/dot_general | solution.py:95
  858.6 19.5 %fusion.227 = bf16[4,1024,3,64]{1,3,2,0:T(8,128)(2,1)} fusion(bf16[4,1024,3,64]{1,3,2,0:T(8,128)(2,1)} %get-tuple-element.406, s32[]{:T(128)S(6)} %copy.135, f32[3,1024,1024]{1,2,0:T(8,128)} %fusion.225, f32[3,1024,1024]{1,2,0:T(8,128)} %copy-done, f32[3,1024]{1,0:T(4,128)S(1)} %dynamic-slice_bitcast_fusion.2, ...), kind=kOutput, calls=%fused_computation.50.clone.1 | convolution fusion | flops 437653504 | bytes 51153920 | tf_op jit(solution)/shard_map/while/body/eval_jaxpr/hqk,khd->qhd/dot_general | solution.py:91
  893.9 19.8 %fusion.228 = bf16[4,1024,3,64]{1,3,2,0:T(8,128)(2,1)} fusion(bf16[4,1024,3,64]{1,3,2,0:T(8,128)(2,1)} %get-tuple-element.407, s32[]{:T(128)S(6)} %copy.135, f32[3,1024,1024]{1,2,0:T(8,128)} %fusion.225, f32[3,1024,1024]{1,2,0:T(8,128)} %copy-done, f32[3,1024]{1,0:T(4,128)S(1)} %dynamic-slice_bitcast_fusion.2, ...), kind=kOutput, calls=%fused_computation.52.clone.1 | convolution fusion | flops 437653504 | bytes 51153920 | tf_op jit(solution)/shard_map/while/body/eval_jaxpr/hqk,qhd->khd/dot_general | solution.py:95
  913.7 19.5 %fusion.227 = bf16[4,1024,3,64]{1,3,2,0:T(8,128)(2,1)} fusion(bf16[4,1024,3,64]{1,3,2,0:T(8,128)(2,1)} %get-tuple-element.406, s32[]{:T(128)S(6)} %copy.135, f32[3,1024,1024]{1,2,0:T(8,128)} %fusion.225, f32[3,1024,1024]{1,2,0:T(8,128)} %copy-done, f32[3,1024]{1,0:T(4,128)S(1)} %dynamic-slice_bitcast_fusion.2, ...), kind=kOutput, calls=%fused_computation.50.clone.1 | convolution fusion | flops 437653504 | bytes 51153920 | tf_op jit(solution)/shard_map/while/body/eval_jaxpr/hqk,khd->qhd/dot_general | solution.py:91
  955.3 12.1 %add_convert_fusion = bf16[4096,768]{1,0:T(8,128)(2,1)} fusion(f32[4096,768]{1,0:T(8,128)} %fusion.154, f32[4096,768]{1,0:T(8,128)} %fusion.155, bf16[4096,192]{0,1:T(8,128)(2,1)S(1)} %bitcast.183, bf16[768,192]{1,0:T(8,128)(2,1)S(1)} %copy-done.28), kind=kOutput, calls=%fused_computation.96 | convolution fusion | flops 1217396736 | bytes 33325056 | tf_op jit(solution)/shard_map/dot_general | solution.py:40
  967.4 10.1 convolution_convert_fusion.6
  983.0 9.8 convolution_convert_fusion.7
  992.9 19.1 %all-to-all-done.3 = bf16[8,768,96]{1,2,0:T(8,128)(2,1)S(1)} async-done(((bf16[8,768,96]{1,2,0:T(8,128)(2,1)}), bf16[8,768,96]{1,2,0:T(8,128)(2,1)S(1)}, u32[]{:S(2)}, u32[]{:S(2)}) %all-to-all-start.3) | async-done | bytes 1179680 | tf_op jit(solution)/shard_map/all_to_all | solution.py:18
  1034.1 11.3 all-to-all-done.2
  1074.5 41.1 %all-reduce.18 = (f32[768]{0:T(1024)S(1)}, f32[768]{0:T(1024)S(1)}, f32[768]{0:T(1024)S(1)}, f32[768]{0:T(1024)S(1)}, f32[768]{0:T(1024)S(1)}, /*index=5*/f32[76...) all-reduce(f32[768]{0:T(1024)S(1)} %dynamic-update-slice.8, ...), channel_id=1, replica_groups=mesh['dp'=8,'tensor'=4] {'dp','tensor'}, use_global_device_ids=true, to_apply=%add.8 | all-reduce | flops 9984 | bytes 79872
  (321 shorter events, 294.3 us)
Async XLA Ops:
  8.0 150.0 %copy-start.42 = (bf16[96,192]{1,0:T(8,128)(2,1)S(1)}, bf16[96,192]{1,0:T(8,128)(2,1)}, u32[]{:S(2)}) copy-start(bf16[96,192]{1,0:T(8,128)(2,1)} %param.26) | copy-start | bytes 110596
  8.0 181.2 %all-gather.7.cloned.1.call-start = ((), (), s32[]{:S(2)}) async-start(), calls=%async_computation.8 | async-start | bytes 7864320 | tf_op jit(solution)/shard_map/all_gather | solution.py:168
  8.8 325.7 %reduce-scatter.5.cloned.1.call-start = ((), (), s32[]{:S(2)}) async-start(), calls=%async_computation.9 | async-start | bytes 7864320 | tf_op jit(solution)/shard_map/reduce_scatter | solution.py:179
  91.5 178.1 %copy-start.23 = (bf16[192,768]{0,1:T(8,128)(2,1)}, bf16[192,768]{0,1:T(8,128)(2,1)S(1)}, u32[]{:S(2)}) copy-start(bf16[192,768]{0,1:T(8,128)(2,1)S(1)} %all_gather.63) | copy-start | bytes 884740
  275.3 59.2 %copy-start.3 = (bf16[1024,768]{1,0:T(8,128)(2,1)S(1)}, bf16[1024,768]{1,0:T(8,128)(2,1)}, u32[]{:S(2)}) copy-start(bf16[1024,768]{1,0:T(8,128)(2,1)} %param.22) | copy-start | bytes 4718596
  275.3 65.6 %all-gather.11.cloned.1.call-start = ((), (), s32[]{:S(2)}) async-start(), calls=%async_computation.11 | async-start | bytes 1327104 | tf_op jit(solution)/shard_map/all_gather | solution.py:153
  275.9 110.0 %all-gather.9.cloned.1.call-start = ((), (), s32[]{:S(2)}) async-start(), calls=%async_computation.10 | async-start | bytes 7864320 | tf_op jit(solution)/shard_map/all_gather | solution.py:191
  339.5 89.8 %all-gather.13.cloned.1.call-start = ((), (), s32[]{:S(2)}) async-start(), calls=%async_computation.12 | async-start | bytes 1327104 | tf_op jit(solution)/shard_map/all_gather | solution.py:154
  340.1 155.7 %reduce-scatter.7.cloned.1.call-start = ((), (), s32[]{:S(2)}) async-start(), calls=%async_computation.13 | async-start | bytes 7864320 | tf_op jit(solution)/shard_map/reduce_scatter | solution.py:197
  438.5 57.3 %copy-start.56 = (f32[768]{0:T(1024)S(1)}, f32[768]{0:T(1024)}, u32[]{:S(2)}) copy-start(f32[768]{0:T(1024)} %get-tuple-element.238) | copy-start | bytes 9220
  438.5 117.0 %all-gather.15.cloned.1.call-start = ((), (), s32[]{:S(2)}) async-start(), calls=%async_computation.14 | async-start | bytes 7864320 | tf_op jit(solution)/shard_map/all_gather | solution.py:224
  438.9 64.6 %copy-start.38 = (f32[1024]{0:T(1024)}, f32[1024]{0:T(1024)S(1)}, u32[]{:S(2)}) copy-start(f32[1024]{0:T(1024)S(1)} %fusion.144) | copy-start | bytes 12292
  509.0 134.2 %reduce-scatter.9.cloned.1.call-start = ((), (), s32[]{:S(2)}) async-start(), calls=%async_computation.15 | async-start | bytes 7864320 | tf_op jit(solution)/shard_map/reduce_scatter | solution.py:233
  555.6 19.1 %copy-start.59 = (bf16[768,768]{1,0:T(8,128)(2,1)S(1)}, bf16[768,768]{1,0:T(8,128)(2,1)}, u32[]{:S(2)}) copy-start(bf16[768,768]{1,0:T(8,128)(2,1)} %all-gather.11.cloned.1.call-done) | copy-start | bytes 3538948
  584.4 63.5 %copy-start.46 = (f32[1024]{0:T(1024)S(1)}, f32[1024]{0:T(1024)}, u32[]{:S(2)}) copy-start(f32[1024]{0:T(1024)} %copy-done.45) | copy-start | bytes 12292
  584.4 116.0 %all-gather.17.cloned.1.call-start = ((), (), s32[]{:S(2)}) async-start(), calls=%async_computation.16 | async-start | bytes 7864320 | tf_op jit(solution)/shard_map/all_gather | solution.py:243
  651.8 48.6 %copy-start.24 = (bf16[192,768]{0,1:T(8,128)(2,1)S(1)}, bf16[192,768]{0,1:T(8,128)(2,1)}, u32[]{:S(2)}) copy-start(bf16[192,768]{0,1:T(8,128)(2,1)} %copy-done.23) | copy-start | bytes 884740
  653.9 472.3 %reduce-scatter.11.cloned.1.call-start = ((), (), s32[]{:S(2)}) async-start(), calls=%async_computation.17 | async-start | bytes 7864320 | tf_op jit(solution)/shard_map/reduce_scatter | solution.py:275
  938.6 10.3 copy-start.16
  942.4 12.9 %copy-start.18 = (bf16[24,8,4,1024]{3,1,2,0:T(8,128)(2,1)}, bf16[24,8,4,1024]{3,1,2,0:T(8,128)(2,1)S(1)}, u32[]{:S(2)}) copy-start(bf16[24,8,4,1024]{3,1,2,0:T(8,128)(2,1)S(1)} %copy.105) | copy-start | bytes 4718596
  977.5 34.5 %all-to-all-start.3 = ((bf16[8,768,96]{1,2,0:T(8,128)(2,1)}), bf16[8,768,96]{1,2,0:T(8,128)(2,1)S(1)}, u32[]{:S(2)}, u32[]{:S(2)}) async-start(bf16[8,768,96]{1,2,0:T(8,128)(2,1)} %bitcast.26), calls=%async_computation.7 | async-start | bytes 2359296 | tf_op jit(solution)/shard_map/all_to_all | solution.py:18
  1013.0 32.4 %all-to-all-start.2 = ((bf16[8,96,768]{2,1,0:T(8,128)(2,1)}), bf16[8,96,768]{2,1,0:T(8,128)(2,1)S(1)}, u32[]{:S(2)}, u32[]{:S(2)}) async-start(bf16[8,96,768]{2,1,0:T(8,128)(2,1)} %bitcast.190), calls=%async_computation.6 | async-start | bytes 2359296 | tf_op jit(solution)/shard_map/all_to_all | solution.py:18
  1016.7 15.3 %slice-start = ((s8[6291456]{0:T(1024)(128)(4,1)}), s8[2097152]{0:T(1024)(128)(4,1)S(1)}, s32[]{:S(2)}) async-start(s8[6291456]{0:T(1024)(128)(4,1)} %bitcast.175), calls=%async_computation.18 | async-start | bytes 4194304
  1045.4 15.5 %all-to-all-start.1 = ((bf16[8,192,96]{2,1,0:T(8,128)(2,1)}), bf16[8,192,96]{2,1,0:T(8,128)(2,1)S(1)}, u32[]{:S(2)}, u32[]{:S(2)}) async-start(bf16[8,192,96]{2,1,0:T(8,128)(2,1)} %bitcast.189), calls=%async_computation.5 | async-start | bytes 786432 | tf_op jit(solution)/shard_map/all_to_all | solution.py:18
  1053.8 12.5 %copy-start.60 = (f32[24]{0:T(128)S(1)}, f32[24]{0:T(128)}, u32[]{:S(2)}) copy-start(f32[24]{0:T(128)} %param.38) | copy-start | bytes 292
  1053.8 12.8 %copy-start.57 = (f32[768]{0:T(1024)S(1)}, f32[768]{0:T(1024)}, u32[]{:S(2)}) copy-start(f32[768]{0:T(1024)} %get-tuple-element.242) | copy-start | bytes 9220
  1061.7 62.3 %all-to-all-start = ((bf16[8,96,576]{2,1,0:T(8,128)(2,1)}), bf16[8,96,576]{2,1,0:T(8,128)(2,1)}, u32[]{:S(2)}, u32[]{:S(2)}) async-start(bf16[8,96,576]{2,1,0:T(8,128)(2,1)} %bitcast.22), calls=%async_computation.4 | async-start | bytes 1966080 | tf_op jit(solution)/shard_map/all_to_all | solution.py:18
  1066.3 54.6 %copy-start.2 = (f32[1024,768]{1,0:T(8,128)S(1)}, f32[1024,768]{1,0:T(8,128)}, u32[]{:S(2)}) copy-start(f32[1024,768]{1,0:T(8,128)} %copy-done.1) | copy-start | bytes 9437188
  1066.3 54.6 %copy-start.36 = (f32[1024]{0:T(1024)S(1)}, f32[1024]{0:T(1024)}, u32[]{:S(2)}) copy-start(f32[1024]{0:T(1024)} %copy-done.35) | copy-start | bytes 12292
  1066.3 54.6 %copy-start.39 = (f32[1024]{0:T(1024)S(1)}, f32[1024]{0:T(1024)}, u32[]{:S(2)}) copy-start(f32[1024]{0:T(1024)} %copy-done.38) | copy-start | bytes 12292
  1066.3 54.6 %copy-start.41 = (f32[1024]{0:T(1024)S(1)}, f32[1024]{0:T(1024)}, u32[]{:S(2)}) copy-start(f32[1024]{0:T(1024)} %copy-done.40) | copy-start | bytes 12292
  1066.3 54.6 %copy-start.48 = (f32[768]{0:T(1024)S(1)}, f32[768]{0:T(1024)}, u32[]{:S(2)}) copy-start(f32[768]{0:T(1024)} %get-tuple-element.239) | copy-start | bytes 9220
  (51 other events, 214.1 us)
Sparse Core Ops, SparseCore 0:
  10.4 50.5 all-gather.6
  275.4 58.9 reduce-scatter.4
  509.2 46.3 all-gather.14
  654.0 46.3 all-gather.16
Sparse Core Ops, SparseCore 1:
  278.0 41.5 all-gather.10
  339.6 46.2 all-gather.8
  387.9 41.3 all-gather.12
  438.6 57.1 reduce-scatter.6
  584.5 58.7 reduce-scatter.8
  967.5 58.7 reduce-scatter.10
where the time goes:
time: 1150 us; the launch traced here: 1140 us
  matrix products  402 us (35%)
  waiting for transfers between devices  358 us (31%)
  blocking collectives  214 us (19%)
  local copies, waits for them, and re-layouts  68.9 us (6%)
  other arithmetic  59.7 us (5%)
  starting transfers between devices  18.3 us (2%)
  between operations  16.6 us (1%)
    unnamed x2, blocking collectives  85.1 us
    dot_general x4, matrix products, attend_backward(): jnp.einsum('hqk,qhd->khd', grad_scores, query_seq, preferred_element_type...  79.2 us
    dot_general x4, matrix products, attend_backward(): jnp.einsum('hqk,khd->qhd', grad_scores, key_seq, preferred_element_type=j...  77.8 us
    dot_general x6, matrix products, matmul(): return jnp.dot(left_side, right_side, preferred_element_type=jnp.float32)  63.5 us
    reduce_scatter x1, waiting for transfers between devices, shards(): lax.psum_scatter(contract_cols(grad_pre, up_weight).astype(jnp.bfloat16),...  58.8 us
    dot_general x6, matrix products, contract_cols(): lax.dot_general(left_side, right_side, (((1,), (1,)), ((), ())), preferre...  58.7 us
    reduce_scatter x1, waiting for transfers between devices, shards(): lax.psum_scatter(matmul(mixed_rows, out_weight).astype(jnp.bfloat16), 'te...  58.1 us
    reduce_scatter x1, waiting for transfers between devices, shards(): lax.psum_scatter(matmul(act_low, down_weight).astype(jnp.bfloat16), 'tens...  56.9 us
  transfers between devices with their start and end apart: 14, of which 10 were waited for; matrix products, arithmetic and copies ran while one was open for 10% of the time, Pallas kernels for 0%

commit v1 on v0

--- a/solution.py
+++ b/solution.py
@@ -6,6 +6,27 @@
 HEAD = 64
 EPSILON = 1e-12
 FLOOR_SCORE = -1e30
+
+
+def ring_gather(x, axis, dim):
+    size, index, rows = (lax.axis_size(axis), lax.axis_index(axis), x.shape[dim])
+    ahead = [(i, (i + 1) % size) for i in range(size)]
+    left = [(i, (i - 1) % size) for i in range(size)]
+    result = jnp.zeros((*x.shape[:dim], size * rows, *x.shape[dim + 1 :]), x.dtype)
+    result = lax.dynamic_update_slice_in_dim(result, x, index * rows, axis=dim)
+    from_left = from_right = x
+    middle = size // 2
+    for step in range(1, middle + 1):
+        from_left = lax.ppermute(from_left, axis, ahead)
+        result = lax.dynamic_update_slice_in_dim(
+            result, from_left, (index - step) % size * rows, axis=dim
+        )
+        if step < size - middle:
+            from_right = lax.ppermute(from_right, axis, left)
+            result = lax.dynamic_update_slice_in_dim(
+                result, from_right, (index + step) % size * rows, axis=dim
+            )
+    return result
 
 
 def cut_along(shard, dim, peers):
@@ -240,7 +261,7 @@
     grad_first, attn_gain_grad, attn_shift_grad = norm_one_back(grad_hidden)
     grad_attn = grad_first.astype(jnp.bfloat16)
     out_bias_grad = jnp.sum(grad_attn.astype(jnp.float32), axis=0)
-    attn_grad_rows = lax.all_gather(grad_attn, "tensor", axis=0, tiled=True)
+    attn_grad_rows = ring_gather(grad_attn, "tensor", 0)
     grad_mixed = contract_cols(attn_grad_rows, out_weight).astype(jnp.bfloat16)
     out_grad = contract_rows(mixed_rows, attn_grad_rows)
     grad_queries, grad_keys, grad_values = lax.map(

time: 1150 us -> 1190 us (1.035)
  matrix products: 402 us -> 433 us
    ppermute x0 -> x3, waiting for transfers between devices: none -> 51.8 us  [the longest x2 51.8 us: ring_gather(): from_left = lax.ppermute(from_left, axis, ahead)]
    all_gather x1 -> x0, waiting for transfers between devices: 46.5 us -> none  [shards(): attn_grad_rows = lax.all_gather(grad_attn, 'tensor', axis=0, tiled=True)]
    dot_general x8, matrix products: 16.8 us -> 34.9 us  [head_scores(): jnp.einsum('qhd,khd->hqk', query_seq, key_seq, preferred_element_type=jnp...]
    dot_general x4, matrix products: 18.7 us -> 34.1 us  [attend_backward(): jnp.einsum('hqk,qhd->khd', prob_low, grad_mix, preferred_element_type=jnp...]
    unnamed x157 -> x159, local copies, waits for them, and re-layouts: 25.3 us -> 27.2 us
  transfers between devices with their start and end apart: 14 -> 16, of which waited for: 10 -> 11; matrix products, arithmetic and copies ran while one was open for 10% -> 10% of each run, Pallas kernels for 0% -> 0%
where the time goes in v1:
time: 1190 us; the launch traced here: 1180 us
  matrix products  433 us (36%)
  waiting for transfers between devices  360 us (30%)
  blocking collectives  217 us (18%)
  local copies, waits for them, and re-layouts  72.7 us (6%)
  other arithmetic  58.6 us (5%)
  starting transfers between devices  19.8 us (2%)
  between operations  16.9 us (1%)
    unnamed x2, blocking collectives  88.3 us
    dot_general x4, matrix products, attend_backward(): jnp.einsum('hqk,qhd->khd', grad_scores, query_seq, preferred_element_type...  79.2 us
    dot_general x4, matrix products, attend_backward(): jnp.einsum('hqk,khd->qhd', grad_scores, key_seq, preferred_element_type=j...  77.8 us
    dot_general x6, matrix products, matmul(): return jnp.dot(left_side, right_side, preferred_element_type=jnp.float32)  63.6 us
    reduce_scatter x1, waiting for transfers between devices, shards(): lax.psum_scatter(contract_cols(grad_pre, up_weight).astype(jnp.bfloat16),...  58.6 us
    reduce_scatter x1, waiting for transfers between devices, shards(): lax.psum_scatter(matmul(mixed_rows, out_weight).astype(jnp.bfloat16), 'te...  58.4 us
    reduce_scatter x1, waiting for transfers between devices, shards(): lax.psum_scatter(matmul(act_low, down_weight).astype(jnp.bfloat16), 'tens...  57 us
    dot_general x6, matrix products, contract_cols(): lax.dot_general(left_side, right_side, (((1,), (1,)), ((), ())), preferre...  55.9 us
  transfers between devices with their start and end apart: 16, of which 11 were waited for; matrix products, arithmetic and copies ran while one was open for 10% of the time, Pallas kernels for 0%

profile of v1, /device:TPU:0, one launch (start us, length us, event | category | flops | bytes accessed | tf_op | source)
XLA Modules:
  0.0 1179.0 jit_solution(11814351240911911207)
XLA Ops:
  15.5 44.0 %all-reduce.19 = (f32[768]{0:T(1024)}, f32[768]{0:T(1024)}, f32[768]{0:T(1024)S(1)}, f32[768]{0:T(1024)S(1)}, f32[768]{0:T(1024)S(1)}, /*index=5*/f32[3072]{0:T(1024)}, f32[768]{0:T(1024)}, f32[768]{0:T(1024)}) all-reduce(f32[768]{0:T(1024)S(1)} %dynamic-update-slice.4, ...), channel_id=1, replica_groups=mesh['dp'=8,'tensor'=4] {'dp','tensor'}, use_global_device_ids=true, to_apply=%add.4 | all-reduce | flops 8448 | bytes 67584
  60.6 31.2 %all_gather.55 = bf16[768,192]{1,0:T(8,128)(2,1)S(1)} all-gather(bf16[96,192]{1,0:T(8,128)(2,1)} %param.26), channel_id=1, replica_groups=mesh['dp'=8,'tensor'=4] {'dp'}, dimensions={0}, use_global_device_ids=true | all-gather | bytes 331776 | tf_op jit(solution)/shard_map/all_gather | solution.py:172
  91.8 33.3 %all_gather.57 = bf16[768,192]{1,0:T(8,128)(2,1)} all-gather(bf16[96,192]{1,0:T(8,128)(2,1)} %param.24), channel_id=1, replica_groups=mesh['dp'=8,'tensor'=4] {'dp'}, dimensions={0}, use_global_device_ids=true | all-gather | bytes 331776 | tf_op jit(solution)/shard_map/all_gather | solution.py:170
  125.0 33.2 %all_gather.59 = bf16[768,192]{1,0:T(8,128)(2,1)} all-gather(bf16[96,192]{1,0:T(8,128)(2,1)} %param.25), channel_id=1, replica_groups=mesh['dp'=8,'tensor'=4] {'dp'}, dimensions={0}, use_global_device_ids=true | all-gather | bytes 331776 | tf_op jit(solution)/shard_map/all_gather | solution.py:171
  158.2 31.0 %all_gather.60 = bf16[192,768]{0,1:T(8,128)(2,1)S(1)} all-gather(bf16[192,96]{0,1:T(8,128)(2,1)S(1)} %copy.88), channel_id=1, replica_groups=mesh['dp'=8,'tensor'=4] {'dp'}, dimensions={1}, use_global_device_ids=true | all-gather | bytes 331776 | tf_op jit(solution)/shard_map/all_gather | solution.py:173
  215.0 49.6 %while.26 = (s32[]{:T(128)}, bf16[4,1024,3,64]{1,3,2,0:T(8,128)(2,1)}, f32[4,3,1024]{2,1,0:T(4,128)}, bf16[4,1024,3,64]{1,3,2,0:T(8,128)(2,1)}, s32[4]{0:T(128)S...) while((s32[]{:T(128)}, ...), condition=%wide.region_3.4_spmd, body=%wide.region_0.3_spmd.sunk | while | flops 843249664 | bytes 39430756 | solution.py:195
  275.8 58.4 %reduce-scatter.5.cloned.1.call-done = bf16[1024,768]{1,0:T(8,128)(2,1)} async-done(((bf16[4096,768]{1,0:T(8,128)(2,1)}), bf16[1024,768]{1,0:T(8,128)(2,1)}) %reduce-scatter.5.cloned.1.call-update) | async-done | bytes 1572880 | tf_op jit(solution)/shard_map/reduce_scatter | solution.py:200
  340.7 44.9 %all-gather.8.cloned.1.call-done = bf16[4096,768]{1,0:T(8,128)(2,1)} async-done(((bf16[1024,768]{1,0:T(8,128)(2,1)}), bf16[4096,768]{1,0:T(8,128)(2,1)}) %all-gather.8.cloned.1.call-update) | async-done | bytes 6291472 | tf_op jit(solution)/shard_map/all_gather | solution.py:212
  385.6 34.8 %multiply_convert_fusion = (bf16[4096,768]{1,0:T(8,128)(2,1)}, f32[4096,768]{1,0:T(8,128)}, f32[4096,768]{1,0:T(8,128)}) fusion(f32[768]{0:T(1024)S(1)} %dynamic_slice.44, bf16[4096,768]{1,0:T(8,128)(2,1)} %all-gather.8.cloned.1.call-done, bf16[768,768]{1,0:T(8,128)(2,1)} %all-gather.10.cloned.1.call-done), kind=kOutput, calls=%fused_computation.97 | convolution fusion | flops 5039456256 | bytes 38931456 | tf_op jit(solution)/shard_map/dot_general | solution.py:51
  429.1 9.2 convolution_convert_fusion.3
  438.7 57.0 %reduce-scatter.7.cloned.1.call-done = bf16[1024,768]{1,0:T(8,128)(2,1)} async-done(((bf16[4096,768]{1,0:T(8,128)(2,1)}), bf16[1024,768]{1,0:T(8,128)(2,1)}) %reduce-scatter.7.cloned.1.call-update) | async-done | bytes 1572880 | tf_op jit(solution)/shard_map/reduce_scatter | solution.py:218
  508.9 46.5 %all-gather.14.cloned.1.call-done = bf16[4096,768]{1,0:T(8,128)(2,1)} async-done(((bf16[1024,768]{1,0:T(8,128)(2,1)}), bf16[4096,768]{1,0:T(8,128)(2,1)}) %all-gather.14.cloned.1.call-update) | async-done | bytes 6291472 | tf_op jit(solution)/shard_map/all_gather | solution.py:245
  555.4 19.1 %convert_reduce_fusion = (f32[768]{0:T(1024)}, bf16[4096,768]{1,0:T(8,128)(2,1)}) fusion(f32[4096,768]{1,0:T(8,128)} %get-tuple-element.253, f32[4096,768]{1,0:T(8,128)} %get-tuple-element.259, f32[768]{0:T(1024)S(1)} %dynamic_slice.44, bf16[4096,768]{1,0:T(8,128)(2,1)} %all-gather.14.cloned.1.call-done, bf16[768,768]{0,1:T(8,128)(2,1)} %all-gather.12.cloned.1.call-done), kind=kOutput, calls=%fused_computation.95 | convolution fusion | flops 4891606016 | bytes 38934528 | tf_op jit(solution)/shard_map/dot_general | solution.py:61
  574.5 9.7 convolution_convert_fusion.1
  584.5 58.6 %reduce-scatter.9.cloned.1.call-done = bf16[1024,768]{1,0:T(8,128)(2,1)} async-done(((bf16[4096,768]{1,0:T(8,128)(2,1)}), bf16[1024,768]{1,0:T(8,128)(2,1)}) %reduce-scatter.9.cloned.1.call-update) | async-done | bytes 1572880 | tf_op jit(solution)/shard_map/reduce_scatter | solution.py:254
  654.3 34.3 %collective-permute-done = bf16[1024,768]{1,0:T(8,128)(2,1)S(1)} collective-permute-done((bf16[1024,768]{1,0:T(8,128)(2,1)S(1)}, bf16[1024,768]{1,0:T(8,128)(2,1)S(1)}, u32[]{:S(2)}, u32[]{:S(2)}) %collective-permute-start) | collective-permute-done | bytes 1572896 | tf_op jit(solution)/shard_map/ppermute | solution.py:20
  691.0 17.5 %collective-permute-done.2 = bf16[1024,768]{1,0:T(8,128)(2,1)} collective-permute-done((bf16[1024,768]{1,0:T(8,128)(2,1)S(1)}, bf16[1024,768]{1,0:T(8,128)(2,1)}, u32[]{:S(2)}, u32[]{:S(2)}) %collective-permute-start.2) | collective-permute-done | bytes 1572896 | tf_op jit(solution)/shard_map/ppermute | solution.py:20
  722.0 254.8 %while.27 = (s32[]{:T(128)}, bf16[4,1024,3,64]{1,3,2,0:T(8,128)(2,1)}, bf16[4,1024,3,64]{1,3,2,0:T(8,128)(2,1)}, bf16[4,1024,3,64]{1,3,2,0:T(8,128)(2,1)}, bf16[...) while((s32[]{:T(128)}, ...), condition=%wide.region_18.19_spmd, body=%wide.region_16.18_spmd.sunk | while | flops 2096047104 | bytes 142458000 | solution.py:267
  738.1 19.8 %fusion.228 = bf16[4,1024,3,64]{1,3,2,0:T(8,128)(2,1)} fusion(bf16[4,1024,3,64]{1,3,2,0:T(8,128)(2,1)} %get-tuple-element.407, s32[]{:T(128)} %get-tuple-element.405, f32[3,1024,1024]{1,2,0:T(8,128)} %fusion.225, f32[3,1024,1024]{1,2,0:T(8,128)} %fusion.226, f32[3,1024]{1,0:T(4,128)S(1)} %dynamic-slice_bitcast_fusion.2, ...), kind=kOutput, calls=%fused_computation.52.clone.1 | convolution fusion | flops 437653504 | bytes 51153920 | tf_op jit(solution)/shard_map/while/body/eval_jaxpr/hqk,qhd->khd/dot_general | solution.py:116
  757.9 19.5 %fusion.227 = bf16[4,1024,3,64]{1,3,2,0:T(8,128)(2,1)} fusion(bf16[4,1024,3,64]{1,3,2,0:T(8,128)(2,1)} %get-tuple-element.406, s32[]{:T(128)} %get-tuple-element.405, f32[3,1024,1024]{1,2,0:T(8,128)} %fusion.225, f32[3,1024,1024]{1,2,0:T(8,128)} %fusion.226, f32[3,1024]{1,0:T(4,128)S(1)} %dynamic-slice_bitcast_fusion.2, ...), kind=kOutput, calls=%fused_computation.50.clone.1 | convolution fusion | flops 437653504 | bytes 51153920 | tf_op jit(solution)/shard_map/while/body/eval_jaxpr/hqk,khd->qhd/dot_general | solution.py:112
  801.7 19.8 %fusion.228 = bf16[4,1024,3,64]{1,3,2,0:T(8,128)(2,1)} fusion(bf16[4,1024,3,64]{1,3,2,0:T(8,128)(2,1)} %get-tuple-element.407, s32[]{:T(128)} %get-tuple-element.405, f32[3,1024,1024]{1,2,0:T(8,128)} %fusion.225, f32[3,1024,1024]{1,2,0:T(8,128)} %fusion.226, f32[3,1024]{1,0:T(4,128)S(1)} %dynamic-slice_bitcast_fusion.2, ...), kind=kOutput, calls=%fused_computation.52.clone.1 | convolution fusion | flops 437653504 | bytes 51153920 | tf_op jit(solution)/shard_map/while/body/eval_jaxpr/hqk,qhd->khd/dot_general | solution.py:116
  821.5 19.5 %fusion.227 = bf16[4,1024,3,64]{1,3,2,0:T(8,128)(2,1)} fusion(bf16[4,1024,3,64]{1,3,2,0:T(8,128)(2,1)} %get-tuple-element.406, s32[]{:T(128)} %get-tuple-element.405, f32[3,1024,1024]{1,2,0:T(8,128)} %fusion.225, f32[3,1024,1024]{1,2,0:T(8,128)} %fusion.226, f32[3,1024]{1,0:T(4,128)S(1)} %dynamic-slice_bitcast_fusion.2, ...), kind=kOutput, calls=%fused_computation.50.clone.1 | convolution fusion | flops 437653504 | bytes 51153920 | tf_op jit(solution)/shard_map/while/body/eval_jaxpr/hqk,khd->qhd/dot_general | solution.py:112
  865.2 19.8 %fusion.228 = bf16[4,1024,3,64]{1,3,2,0:T(8,128)(2,1)} fusion(bf16[4,1024,3,64]{1,3,2,0:T(8,128)(2,1)} %get-tuple-element.407, s32[]{:T(128)} %get-tuple-element.405, f32[3,1024,1024]{1,2,0:T(8,128)} %fusion.225, f32[3,1024,1024]{1,2,0:T(8,128)} %fusion.226, f32[3,1024]{1,0:T(4,128)S(1)} %dynamic-slice_bitcast_fusion.2, ...), kind=kOutput, calls=%fused_computation.52.clone.1 | convolution fusion | flops 437653504 | bytes 51153920 | tf_op jit(solution)/shard_map/while/body/eval_jaxpr/hqk,qhd->khd/dot_general | solution.py:116
  885.0 19.5 %fusion.227 = bf16[4,1024,3,64]{1,3,2,0:T(8,128)(2,1)} fusion(bf16[4,1024,3,64]{1,3,2,0:T(8,128)(2,1)} %get-tuple-element.406, s32[]{:T(128)} %get-tuple-element.405, f32[3,1024,1024]{1,2,0:T(8,128)} %fusion.225, f32[3,1024,1024]{1,2,0:T(8,128)} %fusion.226, f32[3,1024]{1,0:T(4,128)S(1)} %dynamic-slice_bitcast_fusion.2, ...), kind=kOutput, calls=%fused_computation.50.clone.1 | convolution fusion | flops 437653504 | bytes 51153920 | tf_op jit(solution)/shard_map/while/body/eval_jaxpr/hqk,khd->qhd/dot_general | solution.py:112
  928.8 19.8 %fusion.228 = bf16[4,1024,3,64]{1,3,2,0:T(8,128)(2,1)} fusion(bf16[4,1024,3,64]{1,3,2,0:T(8,128)(2,1)} %get-tuple-element.407, s32[]{:T(128)} %get-tuple-element.405, f32[3,1024,1024]{1,2,0:T(8,128)} %fusion.225, f32[3,1024,1024]{1,2,0:T(8,128)} %fusion.226, f32[3,1024]{1,0:T(4,128)S(1)} %dynamic-slice_bitcast_fusion.2, ...), kind=kOutput, calls=%fused_computation.52.clone.1 | convolution fusion | flops 437653504 | bytes 51153920 | tf_op jit(solution)/shard_map/while/body/eval_jaxpr/hqk,qhd->khd/dot_general | solution.py:116
  948.6 19.5 %fusion.227 = bf16[4,1024,3,64]{1,3,2,0:T(8,128)(2,1)} fusion(bf16[4,1024,3,64]{1,3,2,0:T(8,128)(2,1)} %get-tuple-element.406, s32[]{:T(128)} %get-tuple-element.405, f32[3,1024,1024]{1,2,0:T(8,128)} %fusion.225, f32[3,1024,1024]{1,2,0:T(8,128)} %fusion.226, f32[3,1024]{1,0:T(4,128)S(1)} %dynamic-slice_bitcast_fusion.2, ...), kind=kOutput, calls=%fused_computation.50.clone.1 | convolution fusion | flops 437653504 | bytes 51153920 | tf_op jit(solution)/shard_map/while/body/eval_jaxpr/hqk,khd->qhd/dot_general | solution.py:112
  996.8 12.1 %add_convert_fusion = bf16[4096,768]{1,0:T(8,128)(2,1)} fusion(f32[4096,768]{1,0:T(8,128)} %fusion.154, f32[4096,768]{1,0:T(8,128)} %fusion.155, bf16[4096,192]{0,1:T(8,128)(2,1)S(1)} %bitcast.183, bf16[768,192]{1,0:T(8,128)(2,1)S(1)} %copy-done.28), kind=kOutput, calls=%fused_computation.96 | convolution fusion | flops 1217396736 | bytes 33325056 | tf_op jit(solution)/shard_map/dot_general | solution.py:61
  1009.0 10.1 convolution_convert_fusion.6
  1024.4 9.9 convolution_convert_fusion.7
  1034.3 16.2 %all-to-all-done.3 = bf16[8,768,96]{1,2,0:T(8,128)(2,1)S(1)} async-done(((bf16[8,768,96]{1,2,0:T(8,128)(2,1)}), bf16[8,768,96]{1,2,0:T(8,128)(2,1)S(1)}, u32[]{:S(2)}, u32[]{:S(2)}) %all-to-all-start.3) | async-done | bytes 1179680 | tf_op jit(solution)/shard_map/all_to_all | solution.py:39
  1072.5 10.6 all-to-all-done.2
  1112.0 44.3 %all-reduce.18 = (f32[768]{0:T(1024)S(1)}, f32[768]{0:T(1024)S(1)}, f32[768]{0:T(1024)S(1)}, f32[768]{0:T(1024)S(1)}, f32[768]{0:T(1024)S(1)}, /*index=5*/f32[76...) all-reduce(f32[768]{0:T(1024)S(1)} %dynamic-update-slice.8, ...), channel_id=1, replica_groups=mesh['dp'=8,'tensor'=4] {'dp','tensor'}, use_global_device_ids=true, to_apply=%add.8 | all-reduce | flops 9984 | bytes 79872
  (315 shorter events, 338.3 us)
Async XLA Ops:
  8.0 181.2 %all-gather.6.cloned.1.call-start = ((), (), s32[]{:S(2)}) async-start(), calls=%async_computation.8 | async-start | bytes 7864320 | tf_op jit(solution)/shard_map/all_gather | solution.py:189
  8.8 325.5 %reduce-scatter.5.cloned.1.call-start = ((), (), s32[]{:S(2)}) async-start(), calls=%async_computation.9 | async-start | bytes 7864320 | tf_op jit(solution)/shard_map/reduce_scatter | solution.py:200
  91.8 97.5 %copy-start.27 = (bf16[768,192]{1,0:T(8,128)(2,1)}, bf16[768,192]{1,0:T(8,128)(2,1)S(1)}, u32[]{:S(2)}) copy-start(bf16[768,192]{1,0:T(8,128)(2,1)S(1)} %all_gather.55) | copy-start | bytes 884740
  189.2 79.8 %copy-start.23 = (bf16[192,768]{0,1:T(8,128)(2,1)}, bf16[192,768]{0,1:T(8,128)(2,1)S(1)}, u32[]{:S(2)}) copy-start(bf16[192,768]{0,1:T(8,128)(2,1)S(1)} %all_gather.60) | copy-start | bytes 884740
  274.7 59.5 %copy-start.2 = (bf16[1024,768]{1,0:T(8,128)(2,1)S(1)}, bf16[1024,768]{1,0:T(8,128)(2,1)}, u32[]{:S(2)}) copy-start(bf16[1024,768]{1,0:T(8,128)(2,1)} %param.22) | copy-start | bytes 4718596
  274.7 66.0 %all-gather.10.cloned.1.call-start = ((), (), s32[]{:S(2)}) async-start(), calls=%async_computation.11 | async-start | bytes 1327104 | tf_op jit(solution)/shard_map/all_gather | solution.py:174
  275.3 110.3 %all-gather.8.cloned.1.call-start = ((), (), s32[]{:S(2)}) async-start(), calls=%async_computation.10 | async-start | bytes 7864320 | tf_op jit(solution)/shard_map/all_gather | solution.py:212
  339.3 89.8 %all-gather.12.cloned.1.call-start = ((), (), s32[]{:S(2)}) async-start(), calls=%async_computation.12 | async-start | bytes 1327104 | tf_op jit(solution)/shard_map/all_gather | solution.py:175
  339.9 155.7 %reduce-scatter.7.cloned.1.call-start = ((), (), s32[]{:S(2)}) async-start(), calls=%async_computation.13 | async-start | bytes 7864320 | tf_op jit(solution)/shard_map/reduce_scatter | solution.py:218
  438.3 57.4 %copy-start.55 = (f32[768]{0:T(1024)S(1)}, f32[768]{0:T(1024)}, u32[]{:S(2)}) copy-start(f32[768]{0:T(1024)} %get-tuple-element.238) | copy-start | bytes 9220
  438.3 117.1 %all-gather.14.cloned.1.call-start = ((), (), s32[]{:S(2)}) async-start(), calls=%async_computation.14 | async-start | bytes 7864320 | tf_op jit(solution)/shard_map/all_gather | solution.py:245
  438.6 64.7 %copy-start.38 = (f32[1024]{0:T(1024)}, f32[1024]{0:T(1024)S(1)}, u32[]{:S(2)}) copy-start(f32[1024]{0:T(1024)S(1)} %fusion.144) | copy-start | bytes 12292
  508.9 134.2 %reduce-scatter.9.cloned.1.call-start = ((), (), s32[]{:S(2)}) async-start(), calls=%async_computation.15 | async-start | bytes 7864320 | tf_op jit(solution)/shard_map/reduce_scatter | solution.py:254
  555.4 19.1 %copy-start.58 = (bf16[768,768]{1,0:T(8,128)(2,1)S(1)}, bf16[768,768]{1,0:T(8,128)(2,1)}, u32[]{:S(2)}) copy-start(bf16[768,768]{1,0:T(8,128)(2,1)} %all-gather.10.cloned.1.call-done) | copy-start | bytes 3538948
  584.2 63.5 %copy-start.45 = (f32[1024]{0:T(1024)S(1)}, f32[1024]{0:T(1024)}, u32[]{:S(2)}) copy-start(f32[1024]{0:T(1024)} %copy-done.44) | copy-start | bytes 12292
  584.2 582.5 %reduce-scatter.11.cloned.1.call-start = ((), (), s32[]{:S(2)}) async-start(), calls=%async_computation.16 | async-start | bytes 7864320 | tf_op jit(solution)/shard_map/reduce_scatter | solution.py:296
  649.9 38.7 %copy-start.42 = (f32[1024]{0:T(1024)}, f32[1024]{0:T(1024)S(1)}, u32[]{:S(2)}) copy-start(f32[1024]{0:T(1024)S(1)} %negate_multiply_fusion.1) | copy-start | bytes 12292
  652.5 36.0 %collective-permute-start = (bf16[1024,768]{1,0:T(8,128)(2,1)S(1)}, bf16[1024,768]{1,0:T(8,128)(2,1)S(1)}, u32[]{:S(2)}, u32[]{:S(2)}) collective-permute-start(bf16[1024,768]{1,0:T(8,128)(2,1)S(1)} %get-tuple-element.245), channel_id=1, source_target_pairs={{0,1},{1,2},{2,3},{3,0},{4,5},{5,6},{6,7},{7,4},{8,9},{9,10},{10,1... | collective-permute-start | bytes 4718600 | tf_op jit(solution)/shard_map/ppermute | solution.py:20
  652.5 36.8 %collective-permute-start.1 = (bf16[1024,768]{1,0:T(8,128)(2,1)S(1)}, bf16[1024,768]{1,0:T(8,128)(2,1)}, u32[]{:S(2)}, u32[]{:S(2)}) collective-permute-start(bf16[1024,768]{1,0:T(8,128)(2,1)S(1)} %get-tuple-element.245), channel_id=1, source_target_pairs={{0,3},{1,0},{2,1},{3,2},{4,7},{5,4},{6,5},{7,6},{8,11},{9,8},{10,9... | collective-permute-start | bytes 4718600 | tf_op jit(solution)/shard_map/ppermute | solution.py:25
  688.6 19.9 %collective-permute-start.2 = (bf16[1024,768]{1,0:T(8,128)(2,1)S(1)}, bf16[1024,768]{1,0:T(8,128)(2,1)}, u32[]{:S(2)}, u32[]{:S(2)}) collective-permute-start(bf16[1024,768]{1,0:T(8,128)(2,1)S(1)} %collective-permute-done), channel_id=1, source_target_pairs={{0,1},{1,2},{2,3},{3,0},{4,5},{5,6},{6,7},{7,4},{8,9},{9,10},{10,1... | collective-permute-start | bytes 4718600 | tf_op jit(solution)/shard_map/ppermute | solution.py:20
  689.3 23.3 %copy-start.24 = (bf16[192,768]{0,1:T(8,128)(2,1)S(1)}, bf16[192,768]{0,1:T(8,128)(2,1)}, u32[]{:S(2)}) copy-start(bf16[192,768]{0,1:T(8,128)(2,1)} %copy-done.23) | copy-start | bytes 884740
  984.0 12.9 %copy-start.17 = (bf16[24,8,4,1024]{3,1,2,0:T(8,128)(2,1)}, bf16[24,8,4,1024]{3,1,2,0:T(8,128)(2,1)S(1)}, u32[]{:S(2)}) copy-start(bf16[24,8,4,1024]{3,1,2,0:T(8,128)(2,1)S(1)} %copy.105) | copy-start | bytes 4718596
  1019.1 31.5 %all-to-all-start.3 = ((bf16[8,768,96]{1,2,0:T(8,128)(2,1)}), bf16[8,768,96]{1,2,0:T(8,128)(2,1)S(1)}, u32[]{:S(2)}, u32[]{:S(2)}) async-start(bf16[8,768,96]{1,2,0:T(8,128)(2,1)} %bitcast.26), calls=%async_computation.7 | async-start | bytes 2359296 | tf_op jit(solution)/shard_map/all_to_all | solution.py:39
  1051.6 31.6 %all-to-all-start.2 = ((bf16[8,96,768]{2,1,0:T(8,128)(2,1)}), bf16[8,96,768]{2,1,0:T(8,128)(2,1)S(1)}, u32[]{:S(2)}, u32[]{:S(2)}) async-start(bf16[8,96,768]{2,1,0:T(8,128)(2,1)} %bitcast.190), calls=%async_computation.6 | async-start | bytes 2359296 | tf_op jit(solution)/shard_map/all_to_all | solution.py:39
  1055.1 15.2 %slice-start = ((s8[6291456]{0:T(1024)(128)(4,1)}), s8[2097152]{0:T(1024)(128)(4,1)S(1)}, s32[]{:S(2)}) async-start(s8[6291456]{0:T(1024)(128)(4,1)} %bitcast.175), calls=%async_computation.17 | async-start | bytes 4194304
  1083.2 15.2 %all-to-all-start.1 = ((bf16[8,192,96]{2,1,0:T(8,128)(2,1)}), bf16[8,192,96]{2,1,0:T(8,128)(2,1)S(1)}, u32[]{:S(2)}, u32[]{:S(2)}) async-start(bf16[8,192,96]{2,1,0:T(8,128)(2,1)} %bitcast.189), calls=%async_computation.5 | async-start | bytes 786432 | tf_op jit(solution)/shard_map/all_to_all | solution.py:39
  1099.2 65.5 %all-to-all-start = ((bf16[8,96,576]{2,1,0:T(8,128)(2,1)}), bf16[8,96,576]{2,1,0:T(8,128)(2,1)}, u32[]{:S(2)}, u32[]{:S(2)}) async-start(bf16[8,96,576]{2,1,0:T(8,128)(2,1)} %bitcast.22), calls=%async_computation.4 | async-start | bytes 1966080 | tf_op jit(solution)/shard_map/all_to_all | solution.py:39
  1103.7 57.8 %copy-start.1 = (f32[1024,768]{1,0:T(8,128)S(1)}, f32[1024,768]{1,0:T(8,128)}, u32[]{:S(2)}) copy-start(f32[1024,768]{1,0:T(8,128)} %copy-done) | copy-start | bytes 9437188
  1103.7 57.8 %copy-start.36 = (f32[1024]{0:T(1024)S(1)}, f32[1024]{0:T(1024)}, u32[]{:S(2)}) copy-start(f32[1024]{0:T(1024)} %copy-done.35) | copy-start | bytes 12292
  1103.7 57.8 %copy-start.39 = (f32[1024]{0:T(1024)S(1)}, f32[1024]{0:T(1024)}, u32[]{:S(2)}) copy-start(f32[1024]{0:T(1024)} %copy-done.38) | copy-start | bytes 12292
  1103.8 57.8 %copy-start.41 = (f32[1024]{0:T(1024)S(1)}, f32[1024]{0:T(1024)}, u32[]{:S(2)}) copy-start(f32[1024]{0:T(1024)} %copy-done.40) | copy-start | bytes 12292
  1103.8 57.8 %copy-start.47 = (f32[768]{0:T(1024)S(1)}, f32[768]{0:T(1024)}, u32[]{:S(2)}) copy-start(f32[768]{0:T(1024)} %get-tuple-element.239) | copy-start | bytes 9220
  (46 other events, 217.7 us)
Sparse Core Ops, SparseCore 0:
  10.4 50.5 all-gather.5
  274.9 59.3 reduce-scatter.4
  509.0 46.3 all-gather.13
  1009.1 58.6 reduce-scatter.10
Sparse Core Ops, SparseCore 1:
  277.4 41.8 all-gather.9
  339.4 46.2 all-gather.7
  387.7 41.4 all-gather.11
  438.4 57.2 reduce-scatter.6
  584.3 58.7 reduce-scatter.8
